TPU v7x, 8 devices: a whole 2x2x1 slice. The times are simulated.
8 devices in a mesh: rep: 1 (over z), dp: 8 (over x, y, core).
Axes of the slice: x: 2, y: 2, z: 1, core: 2. Of those that a mesh axis runs over, the one named last changes fastest.
Arguments:
- a: bfloat16 [8, 4, 4096, 1280], P(('rep', 'dp'))
- g: bfloat16 [8, 4, 4096, 3072], P(('rep', 'dp'))
Outputs:
- output: bfloat16 [4, 1280, 3072], P('rep')
All inputs are finite; a program needn't handle non-finite values.
Results may differ from a plain program's by a relative error of at most 0.012.
Values are sent between devices in bfloat16 or wider.
A program may use at most 2 GiB of HBM per device.

v0:
```python
import jax
import jax.numpy as jnp


def solution(mesh):
    groups = mesh.shape["rep"]

    def step(a, g):
        a, g = (t.reshape(groups, -1, *t.shape[1:]) for t in (a, g))
        sums = jnp.einsum("rsntd,rsntf->rndf", a, g, preferred_element_type=jnp.float32)
        return sums.astype(jnp.bfloat16).reshape(-1, *sums.shape[2:])

    return step
```

profile of v0, /device:TPU:0, one launch (start us, length us, event | category | flops | bytes accessed | tf_op | source)
XLA Modules:
  0.0 880.6 jit_solution(10287902645567626658)
XLA Ops:
  0.0 142.3 %fusion = f32[4,1280,3072]{2,1,0:T(8,128)} fusion(bf16[1,4,4096,3072]{3,2,1,0:T(8,128)(2,1)} %param.1, bf16[1,4,4096,1280]{3,2,1,0:T(8,128)(2,1)} %param), kind=kOutput, calls=%fused_computation | convolution fusion | flops 128849018880 | bytes 205520896 | tf_op jit(solution)/rsntd,rsntf->rndf/dot_general | solution.py:10
  142.3 738.2 %all-reduce.2 = bf16[4,1280,3072]{2,1,0:T(8,128)(2,1)} all-reduce(f32[4,1280,3072]{2,1,0:T(8,128)} %fusion), channel_id=1, replica_groups=mesh['axis_0'=8] {'axis_0'}, use_global_device_ids=true, to_apply=%add.clone | all-reduce | flops 15728640 | bytes 94371840 | tf_op jit(solution)/rsntd,rsntf->rndf/dot_general | solution.py:10
where the time goes:
time: 881 us
  blocking collectives  738 us (84%)
  matrix products  142 us (16%)
    dot_general x1, blocking collectives, step(): jnp.einsum('rsntd,rsntf->rndf', a, g, preferred_element_type=jnp.float32)  738 us
    dot_general x1, matrix products, step(): jnp.einsum('rsntd,rsntf->rndf', a, g, preferred_element_type=jnp.float32)  142 us

commit v1 on v0

v1 whole, which is shorter than its diff:
```python
import functools

import jax
import jax.numpy as jnp
from jax import lax
from jax.experimental import pallas as pl
from jax.experimental.pallas import tpu as pltpu
from jax.sharding import PartitionSpec as P

MESH = pl.DeviceIdType.MESH
MATS, TOKENS, D, FF = 4, 4096, 1280, 3072
HALF = D // 2
TN = 512
PANELS = FF // TN
ROUNDS = MATS * PANELS // 4
SLOTS = ROUNDS * 4
RB = 80
F32, BF16 = jnp.float32, jnp.bfloat16


def dev(i):
    return {"rep": 0, "dp": i}


def place():
    me = lax.axis_index("dp")
    x, y, core = me // 4, (me // 2) % 2, me % 2
    xn = (1 - x) * 4 + y * 2 + core
    yn = x * 4 + (1 - y) * 2 + core
    partner = x * 4 + y * 2 + (1 - core)
    first = jnp.where(core == 0, xn, yn)
    second = jnp.where(core == 0, yn, xn)
    return x, y, core, first, second, partner


def remote(src, dst, ssem, rsem, to):
    return pltpu.make_async_remote_copy(
        src_ref=src, dst_ref=dst, send_sem=ssem, recv_sem=rsem, device_id=dev(to), device_id_type=MESH
    )


def meet(*others):
    barrier = pltpu.get_barrier_semaphore()
    for other in others:
        pl.semaphore_signal(barrier, inc=1, device_id=dev(other), device_id_type=MESH)
    pl.semaphore_wait(barrier, len(others))


def reduce_kernel(
    a, g, own, abuf, gbuf, acc, dsend, drecv, sbuf, rbuf, fbuf, asem, gsem, dssem, drsem, ssem, rsem, fsem
):
    x, y, core, first, second, partner = place()

    def aload(n, half):
        cols = pl.ds(pl.multiple_of(half * HALF, 128), HALF)
        return pltpu.make_async_copy(a.at[n, :, cols], abuf.at[n % 2, half], asem.at[n % 2, half])

    def where_is(t):
        r, i = t // 4, t % 4
        jx = jnp.where(i < 2, 1 - x, x)
        jy = jnp.where(i % 2 == 0, 1 - y, y)
        q = 4 * r + 2 * jx + jy
        return q // PANELS, q % PANELS

    def gload(t):
        n, p = where_is(t)
        cols = pl.ds(pl.multiple_of(p * TN, 128), TN)
        return pltpu.make_async_copy(g.at[n, :, cols], gbuf.at[t % 2], gsem.at[t % 2])

    def partner_copy(t):
        return remote(dsend.at[t % 2], drecv.at[t % 2], dssem.at[t % 2], drsem.at[t % 2], partner)

    def hop(r, kind, to):
        rp = r % 2
        return remote(sbuf.at[rp, kind], rbuf.at[rp, kind], ssem.at[rp, kind], rsem.at[rp, kind], to)

    def finished(r):
        return pltpu.make_async_copy(fbuf.at[r % 2], own.at[r], fsem.at[r % 2])

    def rows(fn):
        def one(b, _):
            fn(pl.ds(pl.multiple_of(b * RB, 16), RB))
            return 0

        lax.fori_loop(0, HALF // RB, one, 0)

    def finish(r):
        rp = r % 2
        hop(r, 1, first).wait_recv()
        hop(r, 2, second).wait_recv()

        @pl.when(r >= 2)
        def _():
            finished(r - 2).wait()

        def add(s):
            total = acc[3, s, :] + rbuf[rp, 1, s, :].astype(F32) + rbuf[rp, 2, s, :].astype(F32)
            fbuf[rp, s, :] = total.astype(BF16)

        rows(add)
        finished(r).start()

    aload(0, 1 - core).start()
    gload(0).start()
    aload(0, core).start()
    aload(1, 1 - core).start()
    aload(1, core).start()
    meet(first, second, partner)

    def dot(n, half, t):
        return lax.dot_general(
            abuf[n % 2, half], gbuf[t % 2], (((0,), (0,)), ((), ())), preferred_element_type=F32
        )

    def slot(t, _):
        r, i = t // 4, t % 4
        rp = r % 2
        n, _p = where_is(t)

        @pl.when(t == 0)
        def _():
            aload(0, 1 - core).wait()

        for rr, (wait_n, start_n) in {1: (1, None), 2: (None, 2), 3: (2, 3), 4: (3, None)}.items():

            @pl.when(t == 4 * rr)
            def _():
                for half in (0, 1):
                    if wait_n is not None:
                        aload(wait_n, half).wait()
                    if start_n is not None:
                        aload(start_n, half).start()

        gload(t).wait()

        @pl.when(t + 1 < SLOTS)
        def _():
            gload(t + 1).start()

        @pl.when(t >= 2)
        def _():
            partner_copy(t - 2).wait_send()

        dsend[t % 2] = dot(n, 1 - core, t).astype(BF16)
        partner_copy(t).start()

        @pl.when(t == 0)
        def _():
            aload(0, core).wait()

        acc[i] = dot(n, core, t)
        partner_copy(t).wait_recv()

        def add(s):
            acc[i, s, :] = acc[i, s, :] + drecv[t % 2, s, :].astype(F32)

        rows(add)

        def ready(kind):
            @pl.when(r >= 2)
            def _():
                hop(r - 2, kind, first).wait_send()

        def send_raw(kind):
            ready(kind)

            def put(s):
                sbuf[rp, kind, s, :] = acc[i, s, :].astype(BF16)

            rows(put)
            hop(r, kind, first).start()

        @pl.when(i == 0)
        def _():
            send_raw(0)

        @pl.when((i == 1) & (r >= 1))
        def _():
            finish(r - 1)

        @pl.when(i == 1 + core)
        def _():
            send_raw(1)

        @pl.when(i == 2)
        def _():
            hop(r, 0, first).wait_recv()
            ready(2)

            def put(s):
                sbuf[rp, 2, s, :] = (acc[2 - core, s, :] + rbuf[rp, 0, s, :].astype(F32)).astype(BF16)

            rows(put)
            hop(r, 2, second).start()

        return 0

    lax.fori_loop(0, SLOTS, slot, 0)
    finish(ROUNDS - 1)
    for t in (SLOTS - 2, SLOTS - 1):
        partner_copy(t).wait_send()
    for r in (ROUNDS - 2, ROUNDS - 1):
        for kind in range(3):
            hop(r, kind, first).wait_send()
        finished(r).wait()


def gather_kernel(own, out, lsem, ssem, rsem, dssem, drsem):
    x, y, core, first, second, partner = place()
    chip = 2 * x + y
    first_chip = jnp.where(core == 0, 2 * (1 - x) + y, 2 * x + 1 - y)
    second_chip = jnp.where(core == 0, 2 * x + 1 - y, 2 * (1 - x) + y)
    diagonal = 3 - chip

    def part(r, c, half):
        q = 4 * r + c
        return out.at[
            q // PANELS,
            pl.ds(pl.multiple_of(half * HALF, 16), HALF),
            pl.ds(pl.multiple_of((q % PANELS) * TN, 128), TN),
        ]

    def local(r):
        return pltpu.make_async_copy(own.at[r], part(r, chip, core), lsem.at[r])

    def to_first(r):
        return remote(own.at[r], part(r, chip, core), ssem.at[r, 0], rsem.at[r, 0], first)

    def to_second(r):
        return remote(own.at[r], part(r, chip, core), ssem.at[r, 1], rsem.at[r, 1], second)

    def forward(r):
        return remote(part(r, second_chip, core), part(r, second_chip, core), ssem.at[r, 2], rsem.at[r, 2], first)

    def across_own(r):
        return remote(own.at[r], part(r, chip, core), dssem.at[r, 0], drsem.at[r, 0], partner)

    def across(r, k, c):
        return remote(part(r, c, core), part(r, c, core), dssem.at[r, k], drsem.at[r, k], partner)

    meet(first, second, partner)

    def begin(r, _):
        to_first(r).start()
        to_second(r).start()
        across_own(r).start()
        local(r).start()
        return 0

    lax.fori_loop(0, ROUNDS, begin, 0)

    def middle(r, _):
        to_second(r).wait_recv()
        forward(r).start()
        across(r, 1, second_chip).start()
        to_first(r).wait_recv()
        across(r, 2, first_chip).start()
        return 0

    lax.fori_loop(0, ROUNDS, middle, 0)

    def last(r, _):
        forward(r).wait_recv()
        across(r, 3, diagonal).start()
        return 0

    lax.fori_loop(0, ROUNDS, last, 0)

    def drain(r, _):
        local(r).wait()
        to_first(r).wait_send()
        to_second(r).wait_send()
        forward(r).wait_send()
        for k in range(4):
            across(r, k, diagonal).wait()
        return 0

    lax.fori_loop(0, ROUNDS, drain, 0)


def write_kernel(held, out, sem):
    copies = [pltpu.make_async_copy(held.at[n], out.at[n], sem.at[n]) for n in range(MATS)]
    for copy in copies:
        copy.start()
    for copy in copies:
        copy.wait()


def solution(mesh):
    any_space = pl.BlockSpec(memory_space=pl.ANY)
    hbm = pl.BlockSpec(memory_space=pltpu.HBM)
    vmem = pl.BlockSpec(memory_space=pltpu.VMEM)
    dma = pltpu.SemaphoreType.DMA

    def body(a, g):
        own = pl.pallas_call(
            reduce_kernel,
            out_shape=pltpu.HBM((ROUNDS, HALF, TN), BF16),
            in_specs=[any_space] * 2,
            out_specs=hbm,
            scratch_shapes=[
                pltpu.VMEM((2, 2, TOKENS, HALF), BF16),
                pltpu.VMEM((2, TOKENS, TN), BF16),
                pltpu.VMEM((4, HALF, TN), F32),
                pltpu.VMEM((2, HALF, TN), BF16),
                pltpu.VMEM((2, HALF, TN), BF16),
                pltpu.VMEM((2, 3, HALF, TN), BF16),
                pltpu.VMEM((2, 3, HALF, TN), BF16),
                pltpu.VMEM((2, HALF, TN), BF16),
                dma((2, 2)),
                dma((2,)),
                dma((2,)),
                dma((2,)),
                dma((2, 3)),
                dma((2, 3)),
                dma((2,)),
            ],
            compiler_params=pltpu.CompilerParams(
                collective_id=0, has_side_effects=True, vmem_limit_bytes=60 * 2**20
            ),
            name="reduce_scatter",
        )(a[0], g[0])
        held = pl.pallas_call(
            gather_kernel,
            out_shape=pltpu.VMEM((MATS, D, FF), BF16),
            in_specs=[hbm],
            out_specs=vmem,
            scratch_shapes=[
                dma((ROUNDS,)),
                dma((ROUNDS, 3)),
                dma((ROUNDS, 3)),
                dma((ROUNDS, 4)),
                dma((ROUNDS, 4)),
            ],
            compiler_params=pltpu.CompilerParams(
                collective_id=1, has_side_effects=True, vmem_limit_bytes=16 * 2**20
            ),
            name="all_gather",
        )(own)
        return pl.pallas_call(
            write_kernel,
            out_shape=jax.ShapeDtypeStruct((MATS, D, FF), BF16),
            in_specs=[vmem],
            out_specs=any_space,
            scratch_shapes=[dma((MATS,))],
            compiler_params=pltpu.CompilerParams(vmem_limit_bytes=16 * 2**20),
            name="write_out",
        )(held)

    return jax.shard_map(
        body, mesh=mesh, in_specs=P(("rep", "dp")), out_specs=P("rep"), check_vma=False
    )
```

time: 881 us -> 313 us (0.36)
  blocking collectives: 738 us -> 0 us
  Pallas kernels: 0 us -> 311 us
  matrix products: 142 us -> 0 us
    dot_general x1 -> x0, blocking collectives: 738 us -> none  [step(): jnp.einsum('rsntd,rsntf->rndf', a, g, preferred_element_type=jnp.float32)]
    pallas_call x0 -> x3, Pallas kernels: none -> 311 us  [the longest x1 169 us: body(): pl.pallas_call(reduce_kernel, out_shape=pltpu.HBM((ROUNDS, HALF, TN), BF1...]
    dot_general x1 -> x0, matrix products: 142 us -> none  [step(): jnp.einsum('rsntd,rsntf->rndf', a, g, preferred_element_type=jnp.float32)]
where the time goes in v1:
time: 313 us
  Pallas kernels  311 us (99%)
    pallas_call x1, Pallas kernels, body(): pl.pallas_call(reduce_kernel, out_shape=pltpu.HBM((ROUNDS, HALF, TN), BF1...  169 us
    pallas_call x1, Pallas kernels, body(): pl.pallas_call(gather_kernel, out_shape=pltpu.VMEM((MATS, D, FF), BF16),...  132 us
    pallas_call x1, Pallas kernels, body(): pl.pallas_call(write_kernel, out_shape=jax.ShapeDtypeStruct((MATS, D, FF)...  10.6 us

profile of v1, /device:TPU:0, one launch (start us, length us, event | category | flops | bytes accessed | tf_op | source)
XLA Modules:
  0.0 313.3 jit_solution(761400488634486925)
XLA Ops:
  0.0 168.8 %reduce_scatter.1.own = bf16[6,640,512]{2,1,0:T(8,128)(2,1)} custom-call(bf16[4,4096,1280]{2,1,0:T(8,128)(2,1)} %bitcast.2, bf16[4,4096,3072]{2,1,0:T(8,128)(2,1)} %bitcast.1.g), custom_call_target="tpu_custom_call" | custom-call | tf_op jit(solution)/shard_map/reduce_scatter/pallas_call | solution.py:296
  168.8 0.0 copy-start
  168.8 2.1 copy-done
  170.9 131.8 %all_gather.1.held = bf16[4,1280,3072]{2,1,0:T(8,128)(2,1)S(1)} custom-call(bf16[6,640,512]{2,1,0:T(8,128)(2,1)S(1)} %copy-done), custom_call_target="tpu_custom_call" | custom-call | tf_op jit(solution)/shard_map/all_gather/pallas_call | solution.py:323
  302.7 10.6 %write_out.1 = bf16[4,1280,3072]{2,1,0:T(8,128)(2,1)} custom-call(bf16[4,1280,3072]{2,1,0:T(8,128)(2,1)S(1)} %all_gather.1.held), custom_call_target="tpu_custom_call" | custom-call | tf_op jit(solution)/shard_map/write_out/pallas_call | solution.py:340
Async XLA Ops:
  168.8 2.1 copy-start

commit v2 on v0

v2 whole, which is shorter than its diff:
```python
import functools

import jax
import jax.numpy as jnp
from jax import lax
from jax.experimental import pallas as pl
from jax.experimental.pallas import tpu as pltpu
from jax.sharding import PartitionSpec as P

MESH = pl.DeviceIdType.MESH
MATS, TOKENS, D, FF = 4, 4096, 1280, 3072
HALF = D // 2
TN = 512
PANELS = FF // TN
ROUNDS = MATS * PANELS // 4
SLOTS = ROUNDS * 4
RB = 80
F32, BF16 = jnp.float32, jnp.bfloat16
S_AT = (3, 7, 11, 15, 19, 22)
O_AT = (6, 10, 14, 18, 22, 25)
AG_AT = (
    *((0, 0, 8), (0, 1, 11), (0, 2, 14), (0, 3, 14), (0, 4, 24), (1, 0, 15), (1, 1, 18)),
    *((2, 0, 24), (3, 0, 24), (4, 0, 24), (1, 2, 24), (2, 1, 24), (3, 1, 24), (4, 1, 24), (1, 3, 24)),
    *((5, 0, 25), (5, 1, 25), (2, 2, 26), (2, 3, 26), (3, 2, 26), (3, 3, 26), (4, 2, 26), (4, 3, 26), (5, 2, 26), (5, 3, 26)),
    *((1, 4, 27), (2, 4, 27), (3, 4, 27), (4, 4, 27), (5, 4, 27)),
)


def dev(i):
    return {"rep": 0, "dp": i}


def place():
    me = lax.axis_index("dp")
    x, y, core = me // 4, (me // 2) % 2, me % 2
    xn = (1 - x) * 4 + y * 2 + core
    yn = x * 4 + (1 - y) * 2 + core
    partner = x * 4 + y * 2 + (1 - core)
    first = jnp.where(core == 0, xn, yn)
    second = jnp.where(core == 0, yn, xn)
    return x, y, core, first, second, partner


def remote(src, dst, ssem, rsem, to):
    return pltpu.make_async_remote_copy(
        src_ref=src, dst_ref=dst, send_sem=ssem, recv_sem=rsem, device_id=dev(to), device_id_type=MESH
    )


def meet(*others):
    barrier = pltpu.get_barrier_semaphore()
    for other in others:
        pl.semaphore_signal(barrier, inc=1, device_id=dev(other), device_id_type=MESH)
    pl.semaphore_wait(barrier, len(others))


def chips(x, y, core):
    xc, yc = 2 * (1 - x) + y, 2 * x + 1 - y
    return 2 * x + y, jnp.where(core == 0, xc, yc), jnp.where(core == 0, yc, xc)


class Gather:
    def __init__(self, sems, part, own):
        self.ssem, self.rsem, self.dssem, self.drsem = sems
        self.part, self.own = part, own
        self.x, self.y, self.core, self.first, self.second, self.partner = place()
        self.chip, self.first_chip, self.second_chip = chips(self.x, self.y, self.core)

    def chip_copy(self, src, c, r, kind, to):
        return remote(src, self.part(r, c, self.core), self.ssem.at[r, kind], self.rsem.at[r, kind], to)

    def to_first(self, r):
        return self.chip_copy(self.own(r), self.chip, r, 0, self.first)

    def to_second(self, r):
        return self.chip_copy(self.own(r), self.chip, r, 1, self.second)

    def forward(self, r):
        return self.chip_copy(self.part(r, self.second_chip, self.core), self.second_chip, r, 2, self.first)

    def across_own(self, r):
        return remote(
            self.own(r), self.part(r, self.chip, self.core), self.dssem.at[r, 0], self.drsem.at[r, 0], self.partner
        )

    def across(self, r, k, c):
        part = self.part(r, c, self.core)
        return remote(part, part, self.dssem.at[r, k], self.drsem.at[r, k], self.partner)

    def drain(self, r):
        self.to_first(r).wait_send()
        self.to_second(r).wait_send()
        self.forward(r).wait_send()
        for k in range(4):
            self.across(r, k, self.chip).wait()


def sum_kernel(
    a,
    g,
    out,
    abuf,
    gbuf,
    acc,
    dsend,
    drecv,
    sbuf,
    rbuf_d,
    rbuf_f,
    rbuf_s,
    asem,
    gsem,
    dssem,
    drsem,
    ssem,
    rsem,
    *gsems,
):
    x, y, core, first, second, partner = place()
    chip, first_chip, second_chip = chips(x, y, core)

    def part(r, c, half):
        q = 4 * r + c
        return out.at[
            q // PANELS,
            pl.ds(pl.multiple_of(half * HALF, 16), HALF),
            pl.ds(pl.multiple_of((q % PANELS) * TN, 128), TN),
        ]

    gather = Gather(gsems, part, lambda r: part(r, chip, core))

    def where_is(t):
        r, i = t // 4, t % 4
        jx = jnp.where(i < 2, 1 - x, x)
        jy = jnp.where(i % 2 == 0, 1 - y, y)
        q = 4 * r + 2 * jx + jy
        return q // PANELS, q % PANELS

    def aload(t, mine):
        n, _ = where_is(t)
        half = core if mine else 1 - core
        cols = pl.ds(pl.multiple_of(half * HALF, 128), HALF)
        return pltpu.make_async_copy(a.at[n, :, cols], abuf.at[int(mine)], asem.at[int(mine)])

    def gload(t):
        n, p = where_is(t)
        cols = pl.ds(pl.multiple_of(p * TN, 128), TN)
        return pltpu.make_async_copy(g.at[n, :, cols], gbuf.at[t % 2], gsem.at[t % 2])

    def partner_copy(t):
        return remote(dsend, drecv.at[t % 2], dssem, drsem.at[t % 2], partner)

    def hop(r, kind):
        depth, rbuf = ((2, rbuf_d), (3, rbuf_f), (3, rbuf_s))[kind]
        return remote(
            sbuf.at[r % 2, kind],
            rbuf.at[r % depth],
            ssem.at[r % 2, kind],
            rsem.at[r % depth, kind],
            second if kind == 2 else first,
        )

    def rows(fn):
        def one(b, _):
            fn(pl.ds(pl.multiple_of(b * RB, 16), RB))
            return 0

        lax.fori_loop(0, HALF // RB, one, 0)

    def ready(r, kind):
        @pl.when(r >= 2)
        def _():
            hop(r - 2, kind).wait_send()

    def pass_on(r):
        hop(r, 0).wait_recv()
        if r >= 2:
            hop(r - 2, 2).wait_send()

        def put(s):
            sbuf[r % 2, 2, s, :] = (acc[1, s, :] + rbuf_d[r % 2, s, :].astype(F32)).astype(BF16)

        rows(put)
        hop(r, 2).start()

    def finish(r):
        hop(r, 1).wait_recv()
        hop(r, 2).wait_recv()
        done = part(r, chip, core)

        def add(s):
            total = acc[2, s, :] + rbuf_f[r % 3, s, :].astype(F32) + rbuf_s[r % 3, s, :].astype(F32)
            done[s, :] = total.astype(BF16)

        rows(add)

    def spread(r, kind):
        if kind == 0:
            gather.to_first(r).start()
            gather.across_own(r).start()
        elif kind == 1:
            gather.to_second(r).start()
        elif kind == 2:
            gather.to_second(r).wait_recv()
            gather.forward(r).start()
            gather.across(r, 1, second_chip).start()
        elif kind == 3:
            gather.to_first(r).wait_recv()
            gather.across(r, 2, first_chip).start()
        else:
            gather.forward(r).wait_recv()
            gather.across(r, 3, 3 - chip).start()

    actions = [(t, functools.partial(finish, r)) for r, t in enumerate(O_AT)]
    actions += [(t, functools.partial(pass_on, r)) for r, t in enumerate(S_AT)]
    actions += [(t, functools.partial(spread, r, kind)) for r, kind, t in AG_AT]
    actions.sort(key=lambda action: action[0])

    aload(0, False).start()
    gload(0).start()
    aload(0, True).start()
    meet(first, second, partner)

    def dot(mine, t):
        return lax.dot_general(
            abuf[int(mine)], gbuf[t % 2], (((0,), (0,)), ((), ())), preferred_element_type=F32
        )

    def slot(t, _):
        r, i = t // 4, t % 4
        rp = r % 2
        aload(t, False).wait()
        gload(t).wait()

        @pl.when(t + 1 < SLOTS)
        def _():
            gload(t + 1).start()

        @pl.when(t >= 1)
        def _():
            partner_copy(t - 1).wait_send()

        dsend[...] = dot(False, t).astype(BF16)
        partner_copy(t).start()

        @pl.when(t + 1 < SLOTS)
        def _():
            aload(t + 1, False).start()

        aload(t, True).wait()
        kept = jnp.where(i == 3, 2, jnp.where(i == 2 - core, 1, 0))
        acc[kept] = dot(True, t)

        @pl.when(t + 1 < SLOTS)
        def _():
            aload(t + 1, True).start()

        partner_copy(t).wait_recv()

        def add(s):
            acc[kept, s, :] = acc[kept, s, :] + drecv[t % 2, s, :].astype(F32)

        rows(add)

        def send_raw(kind):
            ready(r, kind)

            def put(s):
                sbuf[rp, kind, s, :] = acc[0, s, :].astype(BF16)

            rows(put)
            hop(r, kind).start()

        @pl.when(i == 0)
        def _():
            send_raw(0)

        @pl.when(i == 1 + core)
        def _():
            send_raw(1)

        for at, act in actions:
            if at < SLOTS:
                pl.when(t == at)(act)

        return 0

    lax.fori_loop(0, SLOTS, slot, 0)
    for at, act in actions:
        if at >= SLOTS:
            act()
    partner_copy(SLOTS - 1).wait_send()
    for r in (ROUNDS - 2, ROUNDS - 1):
        for kind in range(3):
            hop(r, kind).wait_send()

    def drain(r, _):
        gather.drain(r)
        return 0

    lax.fori_loop(0, ROUNDS, drain, 0)


def write_kernel(held, out, sem):
    copies = [pltpu.make_async_copy(held.at[n], out.at[n], sem.at[n]) for n in range(MATS)]
    for copy in copies:
        copy.start()
    for copy in copies:
        copy.wait()


def solution(mesh):
    any_space = pl.BlockSpec(memory_space=pl.ANY)
    vmem = pl.BlockSpec(memory_space=pltpu.VMEM)
    dma = pltpu.SemaphoreType.DMA

    def body(a, g):
        held = pl.pallas_call(
            sum_kernel,
            out_shape=pltpu.VMEM((MATS, D, FF), BF16),
            in_specs=[any_space] * 2,
            out_specs=vmem,
            scratch_shapes=[
                pltpu.VMEM((2, TOKENS, HALF), BF16),
                pltpu.VMEM((2, TOKENS, TN), BF16),
                pltpu.VMEM((3, HALF, TN), F32),
                pltpu.VMEM((HALF, TN), BF16),
                pltpu.VMEM((2, HALF, TN), BF16),
                pltpu.VMEM((2, 3, HALF, TN), BF16),
                pltpu.VMEM((2, HALF, TN), BF16),
                pltpu.VMEM((3, HALF, TN), BF16),
                pltpu.VMEM((3, HALF, TN), BF16),
                dma((2,)),
                dma((2,)),
                dma,
                dma((2,)),
                dma((2, 3)),
                dma((3, 3)),
                dma((ROUNDS, 3)),
                dma((ROUNDS, 3)),
                dma((ROUNDS, 4)),
                dma((ROUNDS, 4)),
            ],
            compiler_params=pltpu.CompilerParams(
                collective_id=0, has_side_effects=True, vmem_limit_bytes=35_400_000
            ),
            name="sum_and_share",
        )(a[0], g[0])
        return pl.pallas_call(
            write_kernel,
            out_shape=jax.ShapeDtypeStruct((MATS, D, FF), BF16),
            in_specs=[vmem],
            out_specs=any_space,
            scratch_shapes=[dma((MATS,))],
            compiler_params=pltpu.CompilerParams(vmem_limit_bytes=16 * 2**20),
            name="write_out",
        )(held)

    return jax.shard_map(
        body, mesh=mesh, in_specs=P(("rep", "dp")), out_specs=P("rep"), check_vma=False
    )
```

time: 881 us -> 289 us (0.33)
  blocking collectives: 738 us -> 0 us
  Pallas kernels: 0 us -> 289 us
  matrix products: 142 us -> 0 us
    dot_general x1 -> x0, blocking collectives: 738 us -> none  [step(): jnp.einsum('rsntd,rsntf->rndf', a, g, preferred_element_type=jnp.float32)]
    pallas_call x0 -> x2, Pallas kernels: none -> 289 us  [the longest x1 278 us: body(): pl.pallas_call(sum_kernel, out_shape=pltpu.VMEM((MATS, D, FF), BF16), in_...]
    dot_general x1 -> x0, matrix products: 142 us -> none  [step(): jnp.einsum('rsntd,rsntf->rndf', a, g, preferred_element_type=jnp.float32)]
where the time goes in v2:
time: 289 us
  Pallas kernels  289 us (100%)
    pallas_call x1, Pallas kernels, body(): pl.pallas_call(sum_kernel, out_shape=pltpu.VMEM((MATS, D, FF), BF16), in_...  278 us
    pallas_call x1, Pallas kernels, body(): pl.pallas_call(write_kernel, out_shape=jax.ShapeDtypeStruct((MATS, D, FF)...  10.6 us

profile of v2, /device:TPU:0, one launch (start us, length us, event | category | flops | bytes accessed | tf_op | source)
XLA Modules:
  0.0 289.0 jit_solution(7743511384894110259)
XLA Ops:
  0.0 278.4 %sum_and_share.1.held = bf16[4,1280,3072]{2,1,0:T(8,128)(2,1)S(1)} custom-call(bf16[4,4096,1280]{2,1,0:T(8,128)(2,1)} %bitcast.2, bf16[4,4096,3072]{2,1,0:T(8,128)(2,1)} %bitcast.1.g), custom_call_target="tpu_custom_call" | custom-call | tf_op jit(solution)/shard_map/sum_and_share/pallas_call | solution.py:318
  278.4 10.6 %write_out.1 = bf16[4,1280,3072]{2,1,0:T(8,128)(2,1)} custom-call(bf16[4,1280,3072]{2,1,0:T(8,128)(2,1)S(1)} %sum_and_share.1.held), custom_call_target="tpu_custom_call" | custom-call | tf_op jit(solution)/shard_map/write_out/pallas_call | solution.py:349

commit v3 on v2

--- a/solution.py
+++ b/solution.py
@@ -16,13 +16,15 @@
 SLOTS = ROUNDS * 4
 RB = 80
 F32, BF16 = jnp.float32, jnp.bfloat16
-S_AT = (3, 7, 11, 15, 19, 22)
-O_AT = (6, 10, 14, 18, 22, 25)
+TH = TN // 2
+BLOCKS = tuple((rs, cs) for cs in ((0, TH), (TH, TH)) for rs in ((0, 256), (256, HALF - 256)))
+S_AT = ((1, 2), (6, 7), (10, 11), (14, 15), (18, 19), (22, 22))
+O_AT = (4.5, 10, 14, 18, 22, 25)
 AG_AT = (
-    *((0, 0, 8), (0, 1, 11), (0, 2, 14), (0, 3, 14), (0, 4, 24), (1, 0, 15), (1, 1, 18)),
-    *((2, 0, 24), (3, 0, 24), (4, 0, 24), (1, 2, 24), (2, 1, 24), (3, 1, 24), (4, 1, 24), (1, 3, 24)),
-    *((5, 0, 25), (5, 1, 25), (2, 2, 26), (2, 3, 26), (3, 2, 26), (3, 3, 26), (4, 2, 26), (4, 3, 26), (5, 2, 26), (5, 3, 26)),
-    *((1, 4, 27), (2, 4, 27), (3, 4, 27), (4, 4, 27), (5, 4, 27)),
+    *((0, 0, 4.5), (0, 1, 5), (0, 2, 10), (0, 3, 10), (1, 0, 12), (1, 1, 16), (2, 0, 19), (2, 1, 21)),
+    *((3, 0, 23), (3, 1, 24), (4, 0, 24), (4, 1, 24), (0, 4, 24), (5, 0, 25), (5, 1, 25)),
+    *((r, kind, 26) for r in range(1, 6) for kind in (2, 3)),
+    *((r, 4, 27) for r in range(1, 6)),
 )
 
 
@@ -47,11 +49,9 @@
     )
 
 
-def meet(*others):
-    barrier = pltpu.get_barrier_semaphore()
+def greet(*others):
     for other in others:
-        pl.semaphore_signal(barrier, inc=1, device_id=dev(other), device_id_type=MESH)
-    pl.semaphore_wait(barrier, len(others))
+        pl.semaphore_signal(pltpu.get_barrier_semaphore(), inc=1, device_id=dev(other), device_id_type=MESH)
 
 
 def chips(x, y, core):
@@ -93,6 +93,10 @@
         self.forward(r).wait_send()
         for k in range(4):
             self.across(r, k, self.chip).wait()
+
+
+def panel(r, jx, jy):
+    return 4 * r + 2 * ((jx + jy) % 2) + jx
 
 
 def sum_kernel(
@@ -109,9 +113,12 @@
     rbuf_f,
     rbuf_s,
     asem,
+    psem,
     gsem,
     dssem,
     drsem,
+    pssem,
+    prsem,
     ssem,
     rsem,
     *gsems,
@@ -120,7 +127,7 @@
     chip, first_chip, second_chip = chips(x, y, core)
 
     def part(r, c, half):
-        q = 4 * r + c
+        q = panel(r, c // 2, c % 2)
         return out.at[
             q // PANELS,
             pl.ds(pl.multiple_of(half * HALF, 16), HALF),
@@ -131,35 +138,64 @@
 
     def where_is(t):
         r, i = t // 4, t % 4
-        jx = jnp.where(i < 2, 1 - x, x)
-        jy = jnp.where(i % 2 == 0, 1 - y, y)
-        q = 4 * r + 2 * jx + jy
-        return q // PANELS, q % PANELS
+        ends = panel(r, jnp.where(i == 0, 1 - x, x), jnp.where(i == 0, 1 - y, y))
+        mixed = (i == 1) | (i == 2)
+        low = jnp.where(mixed, panel(r, 1 - x, y), ends)
+        high = jnp.where(mixed, panel(r, x, 1 - y), ends)
+        return low, jnp.where(i == 2, TH, 0), high, jnp.where(i == 1, 0, TH)
+
+    def matrix(t):
+        return where_is(t)[0] // PANELS
+
+    def fresh(t):
+        return matrix(t) != matrix(t - 1)
 
     def aload(t, mine):
-        n, _ = where_is(t)
         half = core if mine else 1 - core
         cols = pl.ds(pl.multiple_of(half * HALF, 128), HALF)
-        return pltpu.make_async_copy(a.at[n, :, cols], abuf.at[int(mine)], asem.at[int(mine)])
+        return pltpu.make_async_copy(a.at[matrix(t), :, cols], abuf.at[int(mine)], asem.at[int(mine)])
+
+    def apiece(mine, k):
+        start, size = BLOCKS[k][0]
+        half = core if mine else 1 - core
+        cols = pl.ds(pl.multiple_of(half * HALF + start, 128), size)
+        return pltpu.make_async_copy(a.at[0, :, cols], abuf.at[int(mine), :, pl.ds(start, size)], psem.at[int(mine), k])
 
     def gload(t):
-        n, p = where_is(t)
-        cols = pl.ds(pl.multiple_of(p * TN, 128), TN)
-        return pltpu.make_async_copy(g.at[n, :, cols], gbuf.at[t % 2], gsem.at[t % 2])
+        low, low_at, high, high_at = where_is(t)
+        return [
+            pltpu.make_async_copy(
+                g.at[q // PANELS, :, pl.ds(pl.multiple_of((q % PANELS) * TN + at, 128), TH)],
+                gbuf.at[t % 2, :, pl.ds(k * TH, TH)],
+                gsem.at[t % 2, k],
+            )
+            for k, (q, at) in enumerate(((low, low_at), (high, high_at)))
+        ]
+
+    def partner_piece(k):
+        (r0, rn), (c0, cn) = BLOCKS[k]
+        at = (pl.ds(r0, rn), pl.ds(c0, cn))
+        return remote(dsend.at[at], drecv.at[(0, *at)], pssem.at[k], prsem.at[k], partner)
 
     def partner_copy(t):
         return remote(dsend, drecv.at[t % 2], dssem, drsem.at[t % 2], partner)
 
-    def hop(r, kind):
+    def hop(r, kind, at=(slice(None), slice(None))):
         depth, rbuf = ((2, rbuf_d), (3, rbuf_f), (3, rbuf_s))[kind]
         return remote(
-            sbuf.at[r % 2, kind],
-            rbuf.at[r % depth],
+            sbuf.at[(r % 2, kind, *at)],
+            rbuf.at[(r % depth, *at)],
             ssem.at[r % 2, kind],
             rsem.at[r % depth, kind],
             second if kind == 2 else first,
         )
 
+    def columns(k):
+        return pl.ds(pl.multiple_of(k * TH, 128), TH)
+
+    def half_hop(r, kind, k):
+        return hop(r, kind, (slice(None), columns(k)))
+
     def rows(fn):
         def one(b, _):
             fn(pl.ds(pl.multiple_of(b * RB, 16), RB))
@@ -172,16 +208,18 @@
         def _():
             hop(r - 2, kind).wait_send()
 
-    def pass_on(r):
-        hop(r, 0).wait_recv()
-        if r >= 2:
-            hop(r - 2, 2).wait_send()
+    def pass_on(r, k):
+        if k == 0:
+            hop(r, 0).wait_recv()
+            if r >= 2:
+                hop(r - 2, 2).wait_send()
 
         def put(s):
-            sbuf[r % 2, 2, s, :] = (acc[1, s, :] + rbuf_d[r % 2, s, :].astype(F32)).astype(BF16)
+            total = acc[1, s, columns(k)] + rbuf_d[r % 2, s, columns(k)].astype(F32)
+            sbuf[r % 2, 2, s, columns(k)] = total.astype(BF16)
 
         rows(put)
-        hop(r, 2).start()
+        half_hop(r, 2, k).start()
 
     def finish(r):
         hop(r, 1).wait_recv()
@@ -212,80 +250,141 @@
             gather.across(r, 3, 3 - chip).start()
 
     actions = [(t, functools.partial(finish, r)) for r, t in enumerate(O_AT)]
-    actions += [(t, functools.partial(pass_on, r)) for r, t in enumerate(S_AT)]
+    actions += [(t, functools.partial(pass_on, r, k)) for r, ts in enumerate(S_AT) for k, t in enumerate(ts)]
     actions += [(t, functools.partial(spread, r, kind)) for r, kind, t in AG_AT]
     actions.sort(key=lambda action: action[0])
 
-    aload(0, False).start()
-    gload(0).start()
-    aload(0, True).start()
-    meet(first, second, partner)
-
-    def dot(mine, t):
+    def act_at(t, now):
+        for at, act in actions:
+            if at < SLOTS and at % 1 == now:
+                pl.when(t == int(at))(act)
+
+    def dot(mine, t, at=(slice(None), slice(None))):
         return lax.dot_general(
-            abuf[int(mine)], gbuf[t % 2], (((0,), (0,)), ((), ())), preferred_element_type=F32
+            abuf[int(mine), :, at[0]], gbuf[t % 2, :, at[1]], (((0,), (0,)), ((), ())), preferred_element_type=F32
         )
+
+    greet(first, second, partner)
+    gload(0)[0].start()
+    apiece(False, 0).start()
+    apiece(True, 0).start()
+
+    def block(k):
+        return tuple(pl.ds(*b) for b in BLOCKS[k])
+
+    def send_block(k):
+        at = block(k)
+        partner_piece(k).wait_recv()
+        sbuf[(0, 0, *at)] = (acc[(0, *at)] + drecv[(0, *at)].astype(F32)).astype(BF16)
+        hop(0, 0, at).start()
+
+    for k in range(4):
+        if k == 0:
+            gload(0)[0].wait()
+        if k == 2:
+            gload(0)[1].wait()
+        if k < 2:
+            apiece(False, k).wait()
+        if k == 0:
+            apiece(False, 1).start()
+            apiece(True, 1).start()
+        dsend[block(k)] = dot(False, 0, block(k)).astype(BF16)
+        if k == 0:
+            pl.semaphore_wait(pltpu.get_barrier_semaphore(), 3)
+        partner_piece(k).start()
+        if k > 0:
+            send_block(k - 1)
+        if k < 2:
+            apiece(True, k).wait()
+        if k == 0:
+            gload(0)[1].start()
+        if k == 1:
+            for load in gload(1):
+                load.start()
+        acc[(0, *block(k))] = dot(True, 0, block(k))
+    send_block(3)
+    for k in range(4):
+        partner_piece(k).wait_send()
 
     def slot(t, _):
         r, i = t // 4, t % 4
         rp = r % 2
-        aload(t, False).wait()
-        gload(t).wait()
-
-        @pl.when(t + 1 < SLOTS)
-        def _():
-            gload(t + 1).start()
-
-        @pl.when(t >= 1)
+        more = t + 1 < SLOTS
+
+        @pl.when(fresh(t))
+        def _():
+            aload(t, False).wait()
+
+        for load in gload(t):
+            load.wait()
+
+        @pl.when(more)
+        def _():
+            for load in gload(t + 1):
+                load.start()
+
+        @pl.when(t >= 2)
         def _():
             partner_copy(t - 1).wait_send()
 
         dsend[...] = dot(False, t).astype(BF16)
         partner_copy(t).start()
 
-        @pl.when(t + 1 < SLOTS)
+        @pl.when(more & fresh(t + 1))
         def _():
             aload(t + 1, False).start()
 
-        aload(t, True).wait()
-        kept = jnp.where(i == 3, 2, jnp.where(i == 2 - core, 1, 0))
+        act_at(t, 0.5)
+
+        @pl.when(fresh(t))
+        def _():
+            aload(t, True).wait()
+
+        kept = jnp.where(i == 3, 2, 0)
         acc[kept] = dot(True, t)
 
-        @pl.when(t + 1 < SLOTS)
+        @pl.when(more & fresh(t + 1))
         def _():
             aload(t + 1, True).start()
 
         partner_copy(t).wait_recv()
 
-        def add(s):
-            acc[kept, s, :] = acc[kept, s, :] + drecv[t % 2, s, :].astype(F32)
-
-        rows(add)
-
-        def send_raw(kind):
-            ready(r, kind)
+        @pl.when(i == 0)
+        def _():
+            ready(r, 0)
 
             def put(s):
-                sbuf[rp, kind, s, :] = acc[0, s, :].astype(BF16)
+                sbuf[rp, 0, s, :] = (acc[0, s, :] + drecv[t % 2, s, :].astype(F32)).astype(BF16)
 
             rows(put)
-            hop(r, kind).start()
-
-        @pl.when(i == 0)
-        def _():
-            send_raw(0)
-
-        @pl.when(i == 1 + core)
-        def _():
-            send_raw(1)
-
-        for at, act in actions:
-            if at < SLOTS:
-                pl.when(t == at)(act)
-
+            hop(r, 0).start()
+
+        @pl.when(i == 3)
+        def _():
+            def put(s):
+                acc[2, s, :] = acc[2, s, :] + drecv[t % 2, s, :].astype(F32)
+
+            rows(put)
+
+        @pl.when((i == 1) | (i == 2))
+        def _():
+            @pl.when(i == 1)
+            def _():
+                ready(r, 1)
+
+            def put(s):
+                mine, passed = columns(core), columns(1 - core)
+                raw = acc[0, s, mine] + drecv[t % 2, s, mine].astype(F32)
+                sbuf[rp, 1, s, columns(i - 1)] = raw.astype(BF16)
+                acc[1, s, columns(i - 1)] = acc[0, s, passed] + drecv[t % 2, s, passed].astype(F32)
+
+            rows(put)
+            half_hop(r, 1, i - 1).start()
+
+        act_at(t, 0)
         return 0
 
-    lax.fori_loop(0, SLOTS, slot, 0)
+    lax.fori_loop(1, SLOTS, slot, 0)
     for at, act in actions:
         if at >= SLOTS:
             act()
@@ -331,9 +430,12 @@
                 pltpu.VMEM((3, HALF, TN), BF16),
                 pltpu.VMEM((3, HALF, TN), BF16),
                 dma((2,)),
-                dma((2,)),
+                dma((2, 2)),
+                dma((2, 2)),
                 dma,
                 dma((2,)),
+                dma((4,)),
+                dma((4,)),
                 dma((2, 3)),
                 dma((3, 3)),
                 dma((ROUNDS, 3)),

time: 289 us -> 287 us (level)
  no operation moved by 1% of the time
where the time goes in v3:
time: 287 us
  Pallas kernels  287 us (100%)
    pallas_call x1, Pallas kernels, body(): pl.pallas_call(sum_kernel, out_shape=pltpu.VMEM((MATS, D, FF), BF16), in_...  277 us
    pallas_call x1, Pallas kernels, body(): pl.pallas_call(write_kernel, out_shape=jax.ShapeDtypeStruct((MATS, D, FF)...  10.6 us

profile of v3, /device:TPU:0, one launch (start us, length us, event | category | flops | bytes accessed | tf_op | source)
XLA Modules:
  0.0 287.4 jit_solution(11784962037523906872)
XLA Ops:
  0.0 276.6 %sum_and_share.1.held = bf16[4,1280,3072]{2,1,0:T(8,128)(2,1)S(1)} custom-call(bf16[4,4096,1280]{2,1,0:T(8,128)(2,1)} %bitcast.2, bf16[4,4096,3072]{2,1,0:T(8,128)(2,1)} %bitcast.1.g), custom_call_target="tpu_custom_call" | custom-call | tf_op jit(solution)/shard_map/sum_and_share/pallas_call | solution.py:417
  276.6 10.6 %write_out.1 = bf16[4,1280,3072]{2,1,0:T(8,128)(2,1)} custom-call(bf16[4,1280,3072]{2,1,0:T(8,128)(2,1)S(1)} %sum_and_share.1.held), custom_call_target="tpu_custom_call" | custom-call | tf_op jit(solution)/shard_map/write_out/pallas_call | solution.py:451
